TPU v7x, 128 devices: a whole 4x4x4 slice. The times are simulated.
128 devices in a mesh: tp: 2 (over core), ep: 64 (over z, y, x).
Axes of the slice: x: 4, y: 4, z: 4, core: 2. Of those that a mesh axis runs over, the one named last changes fastest.
Arguments:
- x: bfloat16 [32768, 2048], P(('ep', 'tp'))
- idx: int32 [32768, 6], P(('ep', 'tp'))
- g: float32 [32768, 6], P(('ep', 'tp'))
- slot: int32 [32768, 6], P(('ep', 'tp'))
- ws1: bfloat16 [2048, 2816], P(None, 'tp')
- ws3: bfloat16 [2048, 2816], P(None, 'tp')
- ws2: bfloat16 [2816, 2048], P('tp')
- w1: bfloat16 [64, 2048, 1408], P('ep')
- w3: bfloat16 [64, 2048, 1408], P('ep')
- w2: bfloat16 [64, 1408, 2048], P('ep')
Outputs:
- output: bfloat16 [32768, 2048], P(('ep', 'tp'))
All inputs are finite; a program needn't handle non-finite values.
Results may differ from a plain program's by a relative error of at most 0.001.
Values are sent between devices in bfloat16 or wider.
A program may use at most 1 GiB of HBM per device.

v0:
```python
import jax
import jax.numpy as jnp
from jax import lax
from jax.sharding import PartitionSpec as P


def _swiglu2(x, w1, w3, w2):
    a = jnp.dot(x, w1, preferred_element_type=jnp.float32)
    b = jnp.dot(x, w3, preferred_element_type=jnp.float32)
    h = (jax.nn.silu(a) * b).astype(jnp.bfloat16)
    return jnp.dot(h, w2, preferred_element_type=jnp.float32)


def _experts(xs, w1, w3, w2):
    a = jnp.einsum("erd,edf->erf", xs, w1, preferred_element_type=jnp.float32)
    b = jnp.einsum("erd,edf->erf", xs, w3, preferred_element_type=jnp.float32)
    h = (jax.nn.silu(a) * b).astype(jnp.bfloat16)
    return jnp.einsum("erf,efd->erd", h, w2, preferred_element_type=jnp.float32).astype(jnp.bfloat16)


def _routed(x, idx, g, slot, w1, w3, w2, ep):
    tok, d = x.shape
    k = idx.shape[1]
    el = w1.shape[0]
    e = el * ep
    cap = max(8, (2 * tok * k + 8 * e - 1) // (8 * e) * 8)
    kept = slot >= 0
    pos = jnp.where(kept, idx * cap + slot, e * cap)
    send = jnp.zeros((e * cap, d), jnp.bfloat16).at[pos.reshape(-1)].set(jnp.repeat(x, k, axis=0), mode="drop")
    recv = lax.all_to_all(send.reshape(ep, el, cap, d), "ep", 0, 0, tiled=True)
    xs = jnp.swapaxes(recv, 0, 1).reshape(el, ep * cap, d)
    out = jnp.swapaxes(_experts(xs, w1, w3, w2).reshape(el, ep, cap, d), 0, 1)
    back = lax.all_to_all(out, "ep", 0, 0, tiled=True).reshape(e * cap, d)
    r = jnp.take(back, jnp.where(kept, pos, 0), axis=0)
    gate = jnp.where(kept, g, 0.0)
    acc = jnp.zeros((tok, d), jnp.float32)
    for j in range(k):
        acc = acc + gate[:, j:j + 1] * r[:, j].astype(jnp.float32)
    return acc


def solution(mesh):
    ep = mesh.shape["ep"]
    rows = P(("ep", "tp"), None)

    def body(x, idx, g, slot, ws1, ws3, ws2, w1, w3, w2):
        xg = lax.all_gather(x, "tp", axis=0, tiled=True)
        s = lax.psum_scatter(_swiglu2(xg, ws1, ws3, ws2), "tp", scatter_dimension=0, tiled=True)
        r = _routed(x, idx, g, slot, w1, w3, w2, ep)
        return (x.astype(jnp.float32) + s + r).astype(jnp.bfloat16)

    return jax.shard_map(
        body, mesh=mesh,
        in_specs=(rows, rows, rows, rows, P(None, "tp"), P(None, "tp"), P("tp", None),
                  P("ep", None, None), P("ep", None, None), P("ep", None, None)),
        out_specs=rows, check_vma=False)
```

profile of v0, /device:TPU:13, one launch (start us, length us, event | category | flops | bytes accessed | tf_op | source)
XLA Modules:
  0.0 541.9 jit_solution(642377017369235604)
XLA Ops:
  6.5 6.0 %broadcast_in_dim.32 = bf16[256,6,2048]{2,1,0:T(8,128)(2,1)} broadcast(bf16[256,2048]{1,0:T(8,128)(2,1)} %param.10), dimensions={0,2} | broadcast | bytes 7340032 | tf_op jit(solution)/shard_map/broadcast_in_dim | solution.py:29
  12.5 0.0 copy-start.1
  12.5 0.0 copy-start.3
  12.5 11.1 %reshape.112 = bf16[1536,2048]{1,0:T(8,128)(2,1)} reshape(bf16[256,6,2048]{2,1,0:T(8,128)(2,1)} %broadcast_in_dim.32) | data formatting | bytes 12582912 | tf_op jit(solution)/shard_map/reshape | solution.py:29
  23.6 0.0 copy-done.1
  23.6 0.0 copy-done.3
  23.6 0.1 copy.14
  23.8 0.1 reshape.86
  23.9 17.4 %scatter_custom_fusion = bf16[3072,2048]{1,0:T(8,128)(2,1)} fusion(s32[1536]{0:T(1024)S(1)} %fusion.16, bf16[1536,2048]{1,0:T(8,128)(2,1)} %reshape.112, bf16[]{:T(256)} %constant.16.clone.1), kind=kCustom, calls=%fused_computation.5 | custom fusion | bytes 12583424 | tf_op jit(solution)/shard_map/scatter | solution.py:29
  41.3 172.8 %all_to_all.10 = bf16[64,1,48,2048]{3,2,1,0:T(8,128)(2,1)S(1)} all-to-all(bf16[64,1,48,2048]{3,2,1,0:T(8,128)(2,1)} %bitcast.67), channel_id=1, replica_groups=mesh['tp'=2,'ep'=64] {'ep'}, dimensions={0} | all-to-all | bytes 25165824 | tf_op jit(solution)/shard_map/all_to_all | solution.py:30
  214.1 24.4 %fusion.5 = f32[3072,1408]{1,0:T(8,128)} fusion(bf16[3072,2048]{1,0:T(8,128)(2,1)S(1)} %bitcast.69, bf16[1,2048,1408]{2,1,0:T(8,128)(2,1)} %param.17), kind=kOutput, calls=%fused_computation.9 | convolution fusion | flops 17716740096 | bytes 35651584 | tf_op jit(solution)/shard_map/erd,edf->erf/dot_general | solution.py:15
  238.6 26.0 %multiply_convert_fusion.clone.4 = bf16[3072,1408]{1,0:T(8,128)(2,1)} fusion(f32[3072,1408]{1,0:T(8,128)} %fusion.5, bf16[3072,2048]{1,0:T(8,128)(2,1)S(1)} %bitcast.70, bf16[1,2048,1408]{2,1,0:T(8,128)(2,1)} %param.18), kind=kOutput, calls=%fused_computation.2.clone.clone.clone.1 | convolution fusion | flops 17742692352 | bytes 44302336 | tf_op jit(solution)/shard_map/erd,edf->erf/dot_general | solution.py:16
  264.6 25.3 %convolution_convert_fusion = bf16[3072,2048]{1,0:T(8,128)(2,1)} fusion(bf16[1,1408,2048]{2,1,0:T(8,128)(2,1)} %param.19, bf16[3072,1408]{1,0:T(8,128)(2,1)} %multiply_convert_fusion.clone.4), kind=kOutput, calls=%fused_computation.3 | convolution fusion | flops 17723031552 | bytes 27000832 | tf_op jit(solution)/shard_map/erf,efd->erd/dot_general | solution.py:18
  289.9 14.4 %all-to-all-start.1 = ((bf16[64,1,48,2048]{3,2,1,0:T(8,128)(2,1)}), bf16[64,1,48,2048]{3,2,1,0:T(8,128)(2,1)}, u32[]{:S(2)}, u32[]{:S(2)}) async-start(bf16[64,1,48,2048]{3,2,1,0:T(8,128)(2,1)} %bitcast.68), calls=%async_computation.2 | async-start | bytes 25165824 | tf_op jit(solution)/shard_map/all_to_all | solution.py:33
  304.3 0.0 all-gather.2.cloned.1.call-start
  304.3 0.7 all-gather.2.cloned.1.call-update
  305.0 0.0 reduce-scatter.2.cloned.1.call-start
  305.1 16.6 %all-gather.2.cloned.1.call-done = bf16[512,2048]{1,0:T(8,128)(2,1)} async-done(((bf16[256,2048]{1,0:T(8,128)(2,1)}), bf16[512,2048]{1,0:T(8,128)(2,1)}) %all-gather.2.cloned.1.call-update) | async-done | bytes 2097168 | tf_op jit(solution)/shard_map/all_gather | solution.py:47
  321.7 0.0 copy-start.6
  321.7 8.4 %fusion.20 = f32[512,1408]{1,0:T(8,128)} fusion(bf16[512,2048]{1,0:T(8,128)(2,1)} %all-gather.2.cloned.1.call-done, bf16[2048,1408]{1,0:T(8,128)(2,1)} %param.14), kind=kOutput, calls=%fused_computation.44 | convolution fusion | flops 2952790016 | bytes 10747904 | tf_op jit(solution)/shard_map/dot_general | solution.py:8
  330.1 0.0 copy-done.6
  330.1 0.0 copy-start.2
  330.1 0.0 copy-start.4
  330.1 0.0 copy-start.5
  330.1 13.9 %fusion.15 = f32[512,2048]{1,0:T(8,128)} fusion(bf16[1408,2048]{1,0:T(8,128)(2,1)} %param.16, bf16[512,2048]{1,0:T(8,128)(2,1)S(1)} %copy-done.6, bf16[2048,1408]{1,0:T(8,128)(2,1)} %param.15, f32[512,1408]{1,0:T(8,128)} %fusion.20), kind=kOutput, calls=%fused_computation.32 | convolution fusion | flops 5909905408 | bytes 20709376 | tf_op jit(solution)/shard_map/dot_general | solution.py:11
  344.0 0.0 reduce-scatter.2.cloned.1.call-update
  344.0 0.0 copy-done.2
  344.0 0.0 copy-done.4
  344.1 0.1 copy.16
  344.2 0.1 reshape.102
  344.4 0.0 copy-done.5
  344.4 141.7 %all-to-all-done.1 = bf16[64,1,48,2048]{3,2,1,0:T(8,128)(2,1)} async-done(((bf16[64,1,48,2048]{3,2,1,0:T(8,128)(2,1)}), bf16[64,1,48,2048]{3,2,1,0:T(8,128)(2,1)}, u32[]{:S(2)}, u32[]{:S(2)}) %all-to-all-start.1) | async-done | bytes 12582944 | tf_op jit(solution)/shard_map/all_to_all | solution.py:33
  486.1 19.2 %gather_fusion = bf16[1536,2048]{1,0:T(8,128)(2,1)} fusion(bf16[3072,2048]{1,0:T(8,128)(2,1)} %bitcast.8, s32[2048]{0:T(1024)S(1)} %pad_clamp_fusion), kind=kCustom, calls=%fused_computation | custom fusion | bytes 12589056 | tf_op jit(solution)/shard_map/jit(_take)/gather | solution.py:34
  505.2 10.9 %reshape.101 = bf16[256,6,2048]{2,1,0:T(8,128)(2,1)} reshape(bf16[1536,2048]{1,0:T(8,128)(2,1)} %gather_fusion) | data formatting | bytes 12582912 | tf_op jit(solution)/shard_map/jit(_take)/gather | solution.py:34
  516.1 0.0 copy-start
  516.1 13.4 %copy_select_fusion = bf16[256,6,2048]{2,0,1:T(8,128)(2,1)} fusion(bf16[256,6,2048]{2,1,0:T(8,128)(2,1)} %reshape.101, pred[256,6]{0,1:T(8,128)(4,1)S(1)} %get-tuple-element.5), kind=kLoop, calls=%fused_computation.4 | loop fusion | flops 3145728 | bytes 12584448 | tf_op jit(solution)/shard_map/jit(_take)/select_n | solution.py:34
  529.6 0.0 reduce-scatter.2.cloned.1.call-done
  529.6 0.0 copy-done
  529.6 5.0 fusion.10
  (6 shorter events, 0.1 us)
Async XLA Ops:
  12.5 11.1 %copy-start.1 = (s32[256,6]{0,1:T(8,128)S(1)}, s32[256,6]{0,1:T(8,128)}, u32[]{:S(2)}) copy-start(s32[256,6]{0,1:T(8,128)} %param.13) | copy-start | bytes 18436
  12.5 11.1 %copy-start.3 = (s32[256,6]{0,1:T(8,128)S(1)}, s32[256,6]{0,1:T(8,128)}, u32[]{:S(2)}) copy-start(s32[256,6]{0,1:T(8,128)} %param.11) | copy-start | bytes 18436
  289.9 196.1 %all-to-all-start.1 = ((bf16[64,1,48,2048]{3,2,1,0:T(8,128)(2,1)}), bf16[64,1,48,2048]{3,2,1,0:T(8,128)(2,1)}, u32[]{:S(2)}, u32[]{:S(2)}) async-start(bf16[64,1,48,2048]{3,2,1,0:T(8,128)(2,1)} %bitcast.68), calls=%async_computation.2 | async-start | bytes 25165824 | tf_op jit(solution)/shard_map/all_to_all | solution.py:33
  304.3 17.4 %all-gather.2.cloned.1.call-start = ((), (), s32[]{:S(2)}) async-start(), calls=%async_computation.3 | async-start | bytes 3145728 | tf_op jit(solution)/shard_map/all_gather | solution.py:47
  305.0 224.6 %reduce-scatter.2.cloned.1.call-start = ((), (), s32[]{:S(2)}) async-start(), calls=%async_computation.4 | async-start | bytes 6291456 | tf_op jit(solution)/shard_map/reduce_scatter | solution.py:48
  321.7 8.4 %copy-start.6 = (bf16[512,2048]{1,0:T(8,128)(2,1)S(1)}, bf16[512,2048]{1,0:T(8,128)(2,1)}, u32[]{:S(2)}) copy-start(bf16[512,2048]{1,0:T(8,128)(2,1)} %all-gather.2.cloned.1.call-done) | copy-start | bytes 6291460
  330.1 13.9 %copy-start.2 = (s32[256,6]{0,1:T(8,128)S(1)}, s32[256,6]{0,1:T(8,128)}, u32[]{:S(2)}) copy-start(s32[256,6]{0,1:T(8,128)} %param.13) | copy-start | bytes 18436
  330.1 13.9 %copy-start.4 = (s32[256,6]{0,1:T(8,128)S(1)}, s32[256,6]{0,1:T(8,128)}, u32[]{:S(2)}) copy-start(s32[256,6]{0,1:T(8,128)} %param.11) | copy-start | bytes 18436
  330.1 14.2 %copy-start.5 = (f32[256,6]{0,1:T(8,128)S(1)}, f32[256,6]{0,1:T(8,128)}, u32[]{:S(2)}) copy-start(f32[256,6]{0,1:T(8,128)} %param.12) | copy-start | bytes 18436
  516.1 13.5 %copy-start = (bf16[256,2048]{1,0:T(8,128)(2,1)S(1)}, bf16[256,2048]{1,0:T(8,128)(2,1)}, u32[]{:S(2)}) copy-start(bf16[256,2048]{1,0:T(8,128)(2,1)} %param.10) | copy-start | bytes 3145732
Sparse Core Ops, SparseCore 0:
  306.7 14.9 all-gather.1
  344.1 15.5 reduce-scatter.1
where the time goes:
time: 575 us; the launch traced here: 542 us
  waiting for transfers between devices  183 us (32%)
  blocking collectives  173 us (30%)
  matrix products  98 us (17%)
  local copies, waits for them, and re-layouts  65.1 us (11%)
  other arithmetic  18.5 us (3%)
  starting transfers between devices  14.4 us (3%)
  between operations  13.7 us (2%)
    all_to_all x1, blocking collectives, _routed(): recv = lax.all_to_all(send.reshape(ep, el, cap, d), 'ep', 0, 0, tiled=True)  173 us
    all_to_all x1, waiting for transfers between devices, _routed(): back = lax.all_to_all(out, 'ep', 0, 0, tiled=True).reshape(e * cap, d)  166 us
    gather x2, local copies, waits for them, and re-layouts, _routed(): r = jnp.take(back, jnp.where(kept, pos, 0), axis=0)  30 us
    dot_general x1, matrix products, _experts(): b = jnp.einsum('erd,edf->erf', xs, w3, preferred_element_type=jnp.float32)  26 us
    dot_general x1, matrix products, _experts(): jnp.einsum('erf,efd->erd', h, w2, preferred_element_type=jnp.float32)  25.3 us
    dot_general x1, matrix products, _experts(): a = jnp.einsum('erd,edf->erf', xs, w1, preferred_element_type=jnp.float32)  24.4 us
    scatter x1, local copies, waits for them, and re-layouts, _routed(): jnp.zeros((e * cap, d), jnp.bfloat16).at[pos.reshape(-1)]  17.4 us
    all_gather x1, waiting for transfers between devices, body(): xg = lax.all_gather(x, 'tp', axis=0, tiled=True)  16.7 us
  transfers between devices with their start and end apart: 3, of which 2 were waited for; matrix products, arithmetic and copies ran while one was open for 12% of the time, Pallas kernels for 0%

commit v1 on v0

v1 whole, which is shorter than its diff:
```python
import jax
import jax.numpy as jnp
from jax import lax
from jax.experimental import pallas as pl
from jax.experimental.pallas import tpu as pltpu
from jax.sharding import PartitionSpec as P

MESH = pl.DeviceIdType.MESH
BF = jnp.bfloat16
F32 = jnp.float32

TOK = 256
D = 2048
F = 1408
K = 6
CAP = 48
CH = 16
NC = CAP // CH
NT = F // 128

COLS = ((0, 640), (640, 640), (1280, 768))
ORDER = ((0, 1, 2), (2, 0, 1), (1, 2, 0))
D1, PS, D2, D3, R3, R2, R1 = range(7)
BASE = {D1: 0, PS: 9, D2: 18, D3: 45, R3: 72, R2: 99, R1: 126}
NSEM = 126 + 108


def _sem(stage, c, p, i, k=0):
    if stage == R1:
        return BASE[R1] + ((c * 3 + p) * 3 + i - 1) * 4 + k
    return BASE[stage] + (c * 3 + p) * 3 + i - 1


def _kernel(x, post, posn, gn, ws1, ws3, ws2, w1, w3, w2,
            out, sa, sb, sc, e, q3a, q3b, q3c, q2a, q2b, q2c, h,
            la, lb, lc, pt, pa, pb, pc, ec, hc, r, w13, w2v, hid, gm,
            acc, xs, part, prem, ssem, rsem, lsem, wsem, tsem):
    ep = lax.axis_index("ep")
    tp = lax.axis_index("tp")
    m = (ep // 16, (ep // 4) % 4, ep % 4)
    mz, my, mx = m
    s = (sa, sb, sc)
    q3 = (q3a, q3b, q3c)
    q2 = (q2a, q2b, q2c)
    line = (la, lb, lc)
    pk = (pa, pb, pc)
    cols = tuple(pl.ds(a, b) for a, b in COLS)

    def dev(d, i):
        t = [mz, my, mx]
        t[d] = (t[d] + i) % 4
        return {"ep": t[0] * 16 + t[1] * 4 + t[2]}

    def at(d, i):
        return (m[d] + i) % 4

    def src(d, i):
        return (m[d] + 4 - i) % 4

    def weights(u1, u3, u2):
        cps = []
        for n in range(NT):
            cps.append(pltpu.make_async_copy(u1.at[:, pl.ds(n * 128, 128)], w13.at[n, :, pl.ds(0, 128)], wsem.at[2 * n]))
            cps.append(pltpu.make_async_copy(u3.at[:, pl.ds(n * 128, 128)], w13.at[n, :, pl.ds(128, 128)], wsem.at[2 * n + 1]))
        for n in range(8):
            cps.append(pltpu.make_async_copy(u2.at[:, pl.ds(n * 256, 256)], w2v.at[n], wsem.at[2 * NT + n]))
        return cps

    wshared = weights(ws1, ws3, ws2)
    for c in wshared:
        c.start()
    own_x = pltpu.make_async_copy(x, xs.at[0], lsem.at[0])
    own_x.start()
    own_line = [pltpu.make_async_copy(x.at[:, cols[p]], line[p].at[m[ORDER[p][0]]], lsem.at[1 + p]) for p in range(3)]
    for c in own_line:
        c.start()

    bar = pltpu.get_barrier_semaphore()
    for d in range(3):
        for i in range(1, 4):
            pl.semaphore_signal(bar, inc=1, device_id=dev(d, i), device_id_type=MESH)
    pl.semaphore_signal(bar, inc=1, device_id={"tp": 1 - tp}, device_id_type=MESH)
    pl.semaphore_wait(bar, 10)

    sent = []

    def remote(a, b, stage, c, p, i, where, k=0):
        n = _sem(stage, c, p, i, k)
        cp = pltpu.make_async_remote_copy(src_ref=a, dst_ref=b, send_sem=ssem.at[n], recv_sem=rsem.at[n],
                                          device_id=where, device_id_type=MESH)
        cp.start()
        sent.append(cp)
        return cp

    d1 = []
    for i in (1, 3, 2):
        for p in range(3):
            d = ORDER[p][0]
            d1.append(remote(post, pt.at[d, m[d]], PS, 0, p, i, dev(d, i)))
            d1.append(remote(x.at[:, cols[p]], line[p].at[m[d]], D1, 0, p, i, dev(d, i)))
    xcp = pltpu.make_async_remote_copy(src_ref=x, dst_ref=xs.at[1], send_sem=tsem.at[0], recv_sem=tsem.at[1],
                                       device_id={"tp": 1 - tp}, device_id_type=MESH)
    xcp.start()
    for d in range(3):
        pt[d, m[d]] = post[...]

    def up(rows):
        def body(n, _):
            ab = jnp.dot(rows(), w13[n], preferred_element_type=F32)
            a = ab[:, :128]
            hid[:, pl.ds(pl.multiple_of(n * 128, 128), 128)] = (jax.nn.silu(a) * ab[:, 128:]).astype(BF)
            return 0
        lax.fori_loop(0, NT, body, 0)

    def down(store):
        def body(n, _):
            store(n, jnp.dot(hid[...], w2v[n], preferred_element_type=F32))
            return 0
        lax.fori_loop(0, 8, body, 0)

    def col(n):
        return pl.ds(pl.multiple_of(n * 256, 256), 256)

    own_x.wait()
    for c in wshared:
        c.wait()
    up(lambda: xs[0])

    def own_rows(n, v):
        acc[:, col(n)] = xs[0, :, col(n)].astype(F32) + v
    down(own_rows)

    for c in own_line:
        c.wait()
    for c in d1:
        c.wait_recv()

    ri = lax.broadcasted_iota(jnp.int32, (TOK, TOK), 0)
    ra, rb, rs = ri // 64, (ri // 16) % 4, ri % 16
    ex = (mz * 16 + ra * 4 + rb, ra * 16 + rb * 4 + mx, rb * 16 + my * 4 + ra)

    def pack(c):
        for p in range(3):
            d = ORDER[p][0]
            tgt = ex[p] * CAP + (rs + c * CH)

            def body(k, _, p=p, d=d, tgt=tgt):
                ps = pt[d, k]
                hit = ps[0:1, :] == tgt
                for j in range(1, K):
                    hit = hit | (ps[j:j + 1, :] == tgt)
                oh = jnp.where(hit, 1.0, 0.0).astype(BF)
                v = jnp.dot(oh, line[p][k], preferred_element_type=F32).astype(BF)
                pk[p][c % 2, :, :, k] = v.reshape(4, 4, CH, COLS[p][1])
                return 0
            lax.fori_loop(0, 4, body, 0)

    def s_dst(p, c, b):
        return s[p].at[c, :, b] if p == 1 else s[p].at[c, :, :, b]

    def send_d2(c):
        res = []
        for i in (1, 3, 2):
            for p in range(3):
                d = ORDER[p][1]
                res.append(remote(pk[p].at[c % 2, at(d, i)], s_dst(p, c, m[d]), D2, c, p, i, dev(d, i)))
        loc = []
        for p in range(3):
            d = ORDER[p][1]
            cp = pltpu.make_async_copy(pk[p].at[c % 2, m[d]], s_dst(p, c, m[d]), lsem.at[4 + c * 3 + p])
            cp.start()
            loc.append(cp)
        return res, loc

    def e_at(buf, p, v):
        if p == 0:
            return buf.at[:, :, v, :, cols[0]]
        if p == 1:
            return buf.at[:, v, :, :, cols[1]]
        return buf.at[v, :, :, :, cols[2]]

    def send_d3(c):
        res = []
        for i in (1, 3, 2):
            for p in range(3):
                d = ORDER[p][2]
                res.append(remote(s[p].at[c, at(d, i)], e_at(e.at[c], p, m[d]), D3, c, p, i, dev(d, i)))
        return res

    def load_e(c):
        cps = []
        for p in range(3):
            d = ORDER[p][2]
            cps.append(pltpu.make_async_copy(s[p].at[c, m[d]], e_at(ec, p, m[d]), lsem.at[13 + p * 4]))
            for i in range(1, 4):
                v = src(d, i)
                cps.append(pltpu.make_async_copy(e_at(e.at[c], p, v), e_at(ec, p, v), lsem.at[13 + p * 4 + i]))
        for cp in cps:
            cp.start()
        for cp in cps:
            cp.wait()

    def experts(c, z):
        up(lambda: ec[z].reshape(TOK, D))

        def store(n, v):
            r[c % 2, z, :, :, :, col(n)] = v.astype(BF).reshape(4, 4, CH, 256)
        down(store)

    def send_r3(c):
        res, loc = [], []
        for i in (1, 3, 2):
            for p in range(3):
                d = ORDER[p][2]
                res.append(remote(e_at(r.at[c % 2], p, at(d, i)), q3[p].at[c, m[d]], R3, c, p, i, dev(d, i)))
        for p in range(3):
            d = ORDER[p][2]
            cp = pltpu.make_async_copy(e_at(r.at[c % 2], p, m[d]), q3[p].at[c, m[d]], lsem.at[25 + c * 3 + p])
            cp.start()
            loc.append(cp)
        return res, loc

    def q3_at(p, c, v):
        return q3[p].at[c, :, v] if p == 1 else q3[p].at[c, :, :, v]

    def q2_at(p, c, v):
        return q2[p].at[c, :, v] if p == 2 else q2[p].at[c, v]

    def send_r2(c):
        res = []
        for i in (1, 3, 2):
            for p in range(3):
                d = ORDER[p][1]
                res.append(remote(q3_at(p, c, at(d, i)), q2_at(p, c, m[d]), R2, c, p, i, dev(d, i)))
        return res

    def r1_src(p, c, v, w, own):
        if p == 0:
            return q3a.at[c, :, v, w] if own else q2a.at[c, w, :, v]
        if p == 1:
            return q3b.at[c, :, w, v] if own else q2b.at[c, w, :, v]
        return q3c.at[c, :, v, w] if own else q2c.at[c, :, w, v]

    def h_at(buf, p, v, w):
        if p == 0:
            return buf.at[v, w, :, :, cols[0]]
        if p == 1:
            return buf.at[w, :, v, :, cols[1]]
        return buf.at[:, v, w, :, cols[2]]

    def send_r1(c):
        res = []
        for i in (1, 3, 2):
            for k in range(4):
                for p in range(3):
                    d, d2 = ORDER[p][0], ORDER[p][1]
                    w = src(d2, k)
                    res.append(remote(r1_src(p, c, at(d, i), w, k == 0), h_at(h.at[c], p, m[d], w),
                                      R1, c, p, i, dev(d, i), k))
        return res

    def load_h(c):
        cps = []
        n = 34
        for p in range(3):
            d, d2 = ORDER[p][0], ORDER[p][1]
            for k in range(4):
                w = src(d2, k)
                cps.append(pltpu.make_async_copy(r1_src(p, c, m[d], w, k == 0), h_at(hc, p, m[d], w), lsem.at[n]))
                n += 1
            for i in range(1, 4):
                v = src(d, i)
                if p == 0:
                    a, b = h.at[c, v, :, :, :, cols[0]], hc.at[v, :, :, :, cols[0]]
                elif p == 1:
                    a, b = h.at[c, :, :, v, :, cols[1]], hc.at[:, :, v, :, cols[1]]
                else:
                    a, b = h.at[c, :, v, :, :, cols[2]], hc.at[:, v, :, :, cols[2]]
                cps.append(pltpu.make_async_copy(a, b, lsem.at[n]))
                n += 1
        for cp in cps:
            cp.start()
        for cp in cps:
            cp.wait()

    li = lax.broadcasted_iota(jnp.int32, (TOK, TOK), 1)

    def combine(c):
        def zz(z, _):
            tgt = (z * 16 + li // 16) * CAP + (li % 16 + c * CH)
            g = jnp.zeros((TOK, TOK), F32)
            for j in range(K):
                g = g + jnp.where(posn[:, j:j + 1] == tgt, gn[:, j:j + 1], 0.0)
            g1 = g.astype(BF)
            t = g - g1.astype(F32)
            g2 = t.astype(BF)
            gm[0] = g1
            gm[1] = g2
            gm[2] = (t - g2.astype(F32)).astype(BF)

            def body(n, _):
                b = hc[z, :, :, :, col(n)].reshape(TOK, 256)
                v = jnp.dot(gm[2], b, preferred_element_type=F32)
                v = v + jnp.dot(gm[1], b, preferred_element_type=F32)
                v = v + jnp.dot(gm[0], b, preferred_element_type=F32)
                acc[:, col(n)] = acc[:, col(n)] + v
                return 0
            lax.fori_loop(0, 8, body, 0)
            return 0
        lax.fori_loop(0, 4, zz, 0)

    def got(res):
        for cp in res:
            cp.wait_recv()

    def loop(lo, hi, f):
        def body(z, _):
            f(z)
            return 0
        lax.fori_loop(lo, hi, body, 0)

    pack(0)
    d20, l20 = send_d2(0)
    pack(1)
    d21, l21 = send_d2(1)

    xcp.wait()
    up(lambda: xs[1])

    def other_rows(n, v):
        part[:, col(n)] = v
    down(other_rows)
    pcp = pltpu.make_async_remote_copy(src_ref=part, dst_ref=prem, send_sem=tsem.at[2], recv_sem=tsem.at[3],
                                       device_id={"tp": 1 - tp}, device_id_type=MESH)
    pcp.start()
    wexp = weights(w1.at[0], w3.at[0], w2.at[0])
    for c in wexp:
        c.start()

    got(d20)
    for c in l20:
        c.wait()
    d30 = send_d3(0)
    for c in d20:
        c.wait_send()
    pack(2)
    d22, l22 = send_d2(2)
    got(d21)
    for c in l21:
        c.wait()
    d31 = send_d3(1)
    for c in wexp:
        c.wait()

    got(d30)
    load_e(0)
    loop(0, 4, lambda z: experts(0, z))
    got(d22)
    for c in l22:
        c.wait()
    d32 = send_d3(2)
    r30, k30 = send_r3(0)

    got(d31)
    load_e(1)
    loop(0, 4, lambda z: experts(1, z))
    r31, k31 = send_r3(1)

    got(d32)
    load_e(2)
    for c in r30:
        c.wait_send()
    for c in k30:
        c.wait()
    loop(0, 2, lambda z: experts(2, z))
    got(r30)
    r20 = send_r2(0)
    loop(2, 4, lambda z: experts(2, z))
    r32, k32 = send_r3(2)

    got(r31)
    for c in k31:
        c.wait()
    r21 = send_r2(1)
    got(r20)
    r10 = send_r1(0)
    got(r32)
    for c in k32:
        c.wait()
    r22 = send_r2(2)
    got(r21)
    r11 = send_r1(1)
    got(r10)
    load_h(0)
    combine(0)
    got(r22)
    r12 = send_r1(2)
    got(r11)
    load_h(1)
    combine(1)
    pcp.wait()
    acc[...] = acc[...] + prem[...]
    got(r12)
    load_h(2)
    combine(2)
    out[...] = acc[...].astype(BF)
    done = set(id(c) for c in d20 + r30)
    for c in sent:
        if id(c) not in done:
            c.wait_send()


def _layer(x, post, posn, gn, ws1, ws3, ws2, w1, w3, w2):
    any_ = pl.BlockSpec(memory_space=pl.ANY)
    vm = pl.BlockSpec(memory_space=pltpu.VMEM)

    def blk(n):
        return jax.ShapeDtypeStruct((NC, 4, 4, 4, CH, n), BF)
    per = [blk(b) for _, b in COLS]
    shapes = [jax.ShapeDtypeStruct((TOK, D), BF)] + per + [blk(D)] + per + per + [blk(D)]
    scratch = [pltpu.VMEM((4, TOK, b), BF) for _, b in COLS]
    scratch += [pltpu.VMEM((3, 4, 8, TOK), jnp.int32)]
    scratch += [pltpu.VMEM((2, 4, 4, 4, CH, b), BF) for _, b in COLS]
    scratch += [
        pltpu.VMEM((4, 4, 4, CH, D), BF),
        pltpu.VMEM((4, 4, 4, CH, D), BF),
        pltpu.VMEM((2, 4, 4, 4, CH, D), BF),
        pltpu.VMEM((NT, D, 256), BF),
        pltpu.VMEM((8, F, 256), BF),
        pltpu.VMEM((TOK, F), BF),
        pltpu.VMEM((3, TOK, TOK), BF),
        pltpu.VMEM((TOK, D), F32),
        pltpu.VMEM((2, TOK, D), BF),
        pltpu.VMEM((TOK, D), F32),
        pltpu.VMEM((TOK, D), F32),
        pltpu.SemaphoreType.DMA((NSEM,)),
        pltpu.SemaphoreType.DMA((NSEM,)),
        pltpu.SemaphoreType.DMA((55,)),
        pltpu.SemaphoreType.DMA((2 * NT + 8,)),
        pltpu.SemaphoreType.DMA((4,)),
    ]
    return pl.pallas_call(
        _kernel,
        out_shape=shapes,
        in_specs=[any_, vm, vm, vm] + [any_] * 6,
        out_specs=[vm] + [any_] * (len(shapes) - 1),
        scratch_shapes=scratch,
        compiler_params=pltpu.CompilerParams(collective_id=0, has_side_effects=True, vmem_limit_bytes=67043328),
    )(x, post, posn, gn, ws1, ws3, ws2, w1, w3, w2)[0]


def solution(mesh):
    rows = P(("ep", "tp"), None)

    def body(x, idx, g, slot, ws1, ws3, ws2, w1, w3, w2):
        pos = jnp.where(slot >= 0, idx * CAP + slot, -1)
        posn = jnp.pad(pos, ((0, 0), (0, 2)), constant_values=-1)
        gn = jnp.pad(g, ((0, 0), (0, 2)))
        return _layer(x, posn.T, posn, gn, ws1, ws3, ws2, w1, w3, w2)

    return jax.shard_map(
        body, mesh=mesh,
        in_specs=(rows, rows, rows, rows, P(None, "tp"), P(None, "tp"), P("tp", None),
                  P("ep", None, None), P("ep", None, None), P("ep", None, None)),
        out_specs=rows, check_vma=False)
```

time: 575 us -> 307 us (0.53)
  the two profiles are of different devices: /device:TPU:13 before, /device:TPU:0 now
where the time goes in v1:
time: 307 us
  Pallas kernels  299 us (97%)
  local copies, waits for them, and re-layouts  6.27 us (2%)
    pallas_call x1, Pallas kernels, _layer(): pl.pallas_call(_kernel, out_shape=shapes, in_specs=[any_, vm, vm, vm] + [...  299 us

profile of v1, /device:TPU:0, one launch (start us, length us, event | category | flops | bytes accessed | tf_op | source)
XLA Modules:
  0.0 306.8 jit_solution(14297442727939471352)
XLA Ops:
  0.0 0.7 broadcast_compare_fusion
  0.7 0.7 broadcast_multiply_fusion
  1.4 0.2 copy.20
  1.6 0.1 copy.18
  1.7 0.8 copy.21
  2.6 0.7 pad.9.gn
  3.2 0.8 copy.19
  4.1 0.7 fusion
  4.8 0.7 copy.22.post
  5.4 299.1 %shard_map.100 = (bf16[256,2048]{1,0:T(8,128)(2,1)}, bf16[3,4,4,4,16,640]{5,4,3,2,1,0:T(8,128)(2,1)}, bf16[3,4,4,4,16,640]{5,4,3,2,1,0:T(8,128)(2,1)}, bf16[3,4,...) custom-call(bf16[256,2048]{1,0:T(8,128)(2,1)} %x.5, ...), custom_call_target="tpu_custom_call" | custom-call | tf_op jit(solution)/shard_map/pallas_call | solution.py:442
  304.5 2.3 copy.24
  (1 shorter events, 0.0 us)

commit v2 on v0

v2 whole, which is shorter than its diff:
```python
import jax
import jax.numpy as jnp
from jax import lax
from jax.experimental import pallas as pl
from jax.experimental.pallas import tpu as pltpu
from jax.sharding import PartitionSpec as P

MESH = pl.DeviceIdType.MESH
BF = jnp.bfloat16
F32 = jnp.float32

TOK = 256
D = 2048
F = 1408
K = 6
CAP = 48
CH = 16
NC = CAP // CH
NT = F // 128

COLS = ((0, 640), (640, 640), (1280, 768))
ORDER = ((0, 1, 2), (2, 0, 1), (1, 2, 0))
D1, PS, GS, R1, D2, D3, R3, R2 = range(8)
BASE = {D1: 0, PS: 9, GS: 18, R1: 27, D3: 36, R3: 63, R2: 90, D2: 117}
NSEM = 117 + 108


def _sem(stage, c, p, i, k):
    if stage == D2:
        return BASE[D2] + ((c * 3 + p) * 3 + i - 1) * 4 + k
    return BASE[stage] + (c * 3 + p) * 3 + i - 1


def _kernel(x, idx, slot, g, ws1, ws3, ws2, w1, w3, w2,
            own, sa, sb, sc, e, q3a, q3b, q3c, q2a, q2b, q2c, fr,
            la, lb, lc, pt, gt, pm, gm, wt, pa, pb, pc, oa, ob, oc, ec, qa, qb, qc, r, w13, w2v, hid,
            acc, xs, prem, ssem, rsem, lsem, wsem, tsem):
    ep = lax.axis_index("ep")
    tp = lax.axis_index("tp")
    m = (ep // 16, (ep // 4) % 4, ep % 4)
    mz, my, mx = m
    s = (sa, sb, sc)
    q3 = (q3a, q3b, q3c)
    q2 = (q2a, q2b, q2c)
    line = (la, lb, lc)
    pk = (pa, pb, pc)
    po = (oa, ob, oc)
    qv = (qa, qb, qc)
    cols = tuple(pl.ds(a, b) for a, b in COLS)

    def dev(d, i):
        t = [mz, my, mx]
        t[d] = (t[d] + i) % 4
        return {"ep": t[0] * 16 + t[1] * 4 + t[2]}

    def at(d, i):
        return (m[d] + i) % 4

    def src(d, i):
        return (m[d] + 4 - i) % 4

    def weights(u1, u3, u2):
        cps = []
        for n in range(NT):
            cps.append(pltpu.make_async_copy(u1.at[:, pl.ds(n * 128, 128)], w13.at[n, :, pl.ds(0, 128)], wsem.at[2 * n]))
            cps.append(pltpu.make_async_copy(u3.at[:, pl.ds(n * 128, 128)], w13.at[n, :, pl.ds(128, 128)], wsem.at[2 * n + 1]))
        for n in range(8):
            cps.append(pltpu.make_async_copy(u2.at[:, pl.ds(n * 256, 256)], w2v.at[n], wsem.at[2 * NT + n]))
        return cps

    bar = pltpu.get_barrier_semaphore()
    for d in range(3):
        for i in range(1, 4):
            pl.semaphore_signal(bar, inc=1, device_id=dev(d, i), device_id_type=MESH)
    pl.semaphore_signal(bar, inc=1, device_id={"tp": 1 - tp}, device_id_type=MESH)

    own_x = pltpu.make_async_copy(x, xs.at[0], lsem.at[0])
    own_x.start()
    own_line = [pltpu.make_async_copy(x.at[:, cols[p]], line[p].at[m[ORDER[p][0]]], lsem.at[1 + p]) for p in range(3)]
    for c in own_line:
        c.start()
    pm[...] = jnp.full((8, TOK), -1, jnp.int32)
    gm[...] = jnp.zeros((8, TOK), F32)
    pm[0:K, :] = jnp.where(slot[...] >= 0, idx[...] * CAP + slot[...], -1)
    gm[0:K, :] = g[...]
    for d in range(3):
        pt[d, m[d]] = pm[...]
        gt[d, m[d]] = gm[...]
    pl.semaphore_wait(bar, 10)

    def remote(a, b, stage, c, p, i, where, k=0):
        n = _sem(stage, c, p, i, k)
        return pltpu.make_async_remote_copy(src_ref=a, dst_ref=b, send_sem=ssem.at[n], recv_sem=rsem.at[n],
                                            device_id=where, device_id_type=MESH)

    def local(a, b, n):
        return pltpu.make_async_copy(a, b, lsem.at[n])

    def go(cps):
        for cp in cps:
            cp.start()

    def fin(cps):
        for cp in cps:
            cp.wait()

    def got(cps):
        for cp in cps:
            cp.wait_recv()

    def gone(cps):
        for cp in cps:
            cp.wait_send()

    near = (1, 3, 2)

    d1 = []
    for i in near:
        for p in range(3):
            d = ORDER[p][0]
            d1.append(remote(pm, pt.at[d, m[d]], PS, 0, p, i, dev(d, i)))
            d1.append(remote(gm, gt.at[d, m[d]], GS, 0, p, i, dev(d, i)))
            d1.append(remote(x.at[:, cols[p]], line[p].at[m[d]], D1, 0, p, i, dev(d, i)))
    go(d1)
    xcp = pltpu.make_async_remote_copy(src_ref=x, dst_ref=xs.at[1], send_sem=tsem.at[0], recv_sem=tsem.at[1],
                                       device_id={"tp": 1 - tp}, device_id_type=MESH)
    xcp.start()
    wshared = weights(ws1, ws3, ws2)
    go(wshared)

    def tiles(count, unroll, f):
        def body(q, _):
            for u in range(unroll):
                f(q * unroll + u)
            return 0
        whole = count // unroll
        if whole == 1:
            body(0, 0)
        else:
            lax.fori_loop(0, whole, body, 0)
        for n in range(whole * unroll, count):
            f(n)

    def span(n, w):
        return pl.ds(n * w if isinstance(n, int) else pl.multiple_of(n * w, w), w)

    def up(rows, unroll):
        def f(n):
            ab = jnp.dot(rows(), w13[n], preferred_element_type=F32)
            hid[:, span(n, 128)] = (jax.nn.silu(ab[:, :128]) * ab[:, 128:]).astype(BF)
        tiles(NT, unroll, f)

    def down(store, unroll):
        tiles(8, unroll, lambda n: store(n, jnp.dot(hid[...], w2v[n], preferred_element_type=F32)))

    ri = lax.broadcasted_iota(jnp.int32, (TOK, TOK), 0)
    ra, rb, rs = ri // 64, (ri // 16) % 4, ri % 16
    ex = (mz * 16 + ra * 4 + rb, ra * 16 + rb * 4 + mx, rb * 16 + my * 4 + ra)
    base = tuple(v * CAP + rs for v in ex)

    def picked(c, p, v):
        ps = pt[ORDER[p][0], v] - c * CH
        hit = ps[0:1, :] == base[p]
        for j in range(1, K):
            hit = hit | (ps[j:j + 1, :] == base[p])
        oh = jnp.where(hit, 1.0, 0.0).astype(BF)
        w = jnp.dot(oh, line[p][v], preferred_element_type=F32).astype(BF)
        return w.reshape(4, 4, CH, COLS[p][1])

    def pack(c):
        def body(k, _):
            for p in range(3):
                pk[p][c % 2, k] = picked(c, p, (m[ORDER[p][0]] + k + 1) % 4)
            return 0
        lax.fori_loop(0, 3, body, 0)

    def pack_own():
        def body(c, _):
            for p in range(3):
                po[p][c] = picked(c, p, m[ORDER[p][0]])
            return 0
        lax.fori_loop(0, NC, body, 0)

    def packed(c, p, k):
        return po[p].at[c] if k == 0 else pk[p].at[c % 2, k - 1]

    def s_dst(p, c, b, v):
        return s[p].at[c, :, b, v] if p == 1 else s[p].at[c, :, v, b]

    def d2(c, ks):
        res = []
        for k in ks:
            for i in near:
                for p in range(3):
                    d = ORDER[p][1]
                    res.append(remote(packed(c, p, k).at[at(d, i)], s_dst(p, c, m[d], at(ORDER[p][0], k)),
                                      D2, c, p, i, dev(d, i), k))
        return res

    def d2_own(c, ks):
        res = []
        for k in ks:
            for p in range(3):
                v = m[ORDER[p][1]]
                res.append(local(packed(c, p, k).at[v], s_dst(p, c, v, at(ORDER[p][0], k)), 55 + (c * 3 + p) * 4 + k))
        return res

    def e_at(buf, p, v):
        if p == 0:
            return buf.at[:, :, v, :, cols[0]]
        if p == 1:
            return buf.at[:, v, :, :, cols[1]]
        return buf.at[v, :, :, :, cols[2]]

    def d3(c):
        res = []
        for i in near:
            for p in range(3):
                d = ORDER[p][2]
                res.append(remote(s[p].at[c, at(d, i)], e_at(e.at[c], p, m[d]), D3, c, p, i, dev(d, i)))
        return res

    def load_e(c):
        cps = [local(s[p].at[c, m[ORDER[p][2]]], e_at(ec, p, m[ORDER[p][2]]), 13 + p * 4) for p in range(3)]
        go(cps)
        arrived = d3(c)
        for q, i in enumerate(near):
            for p in range(3):
                arrived[q * 3 + p].wait_recv()
                v = src(ORDER[p][2], i)
                cp = local(e_at(e.at[c], p, v), e_at(ec, p, v), 13 + p * 4 + i)
                cp.start()
                cps.append(cp)
        fin(cps)

    def experts(events):
        def body(b, _):
            for at_b, event in events:
                pl.when(b == at_b)(event)
            z = b % 4
            up(lambda: ec[z].reshape(TOK, D), NT)

            def store(n, v):
                r[(b // 4) % 2, z, :, :, :, span(n, 256)] = v.astype(BF).reshape(4, 4, CH, 256)
            down(store, 8)
            return 0
        lax.fori_loop(0, 4 * NC, body, 0)

    def r3(c):
        res = []
        for i in near:
            for p in range(3):
                d = ORDER[p][2]
                res.append(remote(e_at(r.at[c % 2], p, at(d, i)), q3[p].at[c, m[d]], R3, c, p, i, dev(d, i)))
        return res

    def r3_own(c):
        return [local(e_at(r.at[c % 2], p, m[ORDER[p][2]]), q3[p].at[c, m[ORDER[p][2]]], 25 + c * 3 + p) for p in range(3)]

    def q3_at(p, c, v):
        return q3[p].at[c, :, v] if p == 1 else q3[p].at[c, :, :, v]

    def q2_at(p, c, v):
        return q2[p].at[c, :, v] if p == 2 else q2[p].at[c, v]

    def r2(c):
        res = []
        for i in near:
            for p in range(3):
                d = ORDER[p][1]
                res.append(remote(q3_at(p, c, at(d, i)), q2_at(p, c, m[d]), R2, c, p, i, dev(d, i)))
        return res

    def load_q(c):
        cps = []
        for p in range(3):
            w = m[ORDER[p][1]]
            cps.append(local(q3_at(p, c, w), qv[p].at[w], 34 + p * 4))
        go(cps)
        arrived = r2(c)
        for q, i in enumerate(near):
            for p in range(3):
                arrived[q * 3 + p].wait_recv()
                w = src(ORDER[p][1], i)
                cp = local(q2_at(p, c, w), qv[p].at[w], 34 + p * 4 + i)
                cp.start()
                cps.append(cp)
        fin(cps)

    def add(c, p, i):
        d = ORDER[p][0]
        v = at(d, i)
        ps = pt[d, v] - c * CH
        gs = gt[d, v]
        w = jnp.zeros((TOK, TOK), F32)
        for j in range(K):
            w = w + jnp.where(ps[j:j + 1, :] == base[p], gs[j:j + 1, :], 0.0)
        w1_ = w.astype(BF)
        t = w - w1_.astype(F32)
        w2_ = t.astype(BF)
        w3_ = (t - w2_.astype(F32)).astype(BF)
        rows = qv[p][:, :, v].reshape(TOK, COLS[p][1])
        wt[p, :, 0:TOK] = w1_
        wt[p, :, TOK:2 * TOK] = w2_
        wt[p, :, 2 * TOK:3 * TOK] = w3_
        y = lax.dot_general(wt[p], rows, (((0,), (0,)), ((), ())), preferred_element_type=F32)
        y = (y[2 * TOK:] + y[TOK:2 * TOK]) + y[:TOK]
        acc[i, :, cols[p]] = acc[i, :, cols[p]] + y

    def add_all(c):
        def body(i, _):
            for p in range(3):
                add(c, p, i)
            return 0
        lax.fori_loop(0, 4, body, 0)

    def r1_at(p, i):
        d = ORDER[p][0]
        n = BASE[R1] + p * 3 + i - 1
        return pltpu.make_async_remote_copy(src_ref=acc.at[i, :, cols[p]], dst_ref=fr.at[i, :, cols[p]],
                                            send_sem=ssem.at[n], recv_sem=rsem.at[n],
                                            device_id=dev(d, i), device_id_type=MESH)

    every, rest = (0, 1, 2, 3), (1, 2, 3)
    fin(own_line)
    pack_own()
    for c in range(NC):
        go(d2(c, (0,)))
        go(d2_own(c, (0,)))
    got(d1)
    pack(0)
    go(d2(0, rest))
    go(d2_own(0, rest))

    own_x.wait()
    xcp.wait()
    fin(wshared)

    def shared(k, _):
        up(lambda: xs[k], 4)

        def store(n, v):
            acc[k, :, span(n, 256)] = v
        down(store, 4)
        return 0
    lax.fori_loop(0, 2, shared, 0)
    pcp = pltpu.make_async_remote_copy(src_ref=acc.at[1], dst_ref=prem, send_sem=tsem.at[2], recv_sem=tsem.at[3],
                                       device_id={"tp": 1 - tp}, device_id_type=MESH)
    pcp.start()
    wexp = weights(w1.at[0], w3.at[0], w2.at[0])
    go(wexp)

    pack(1)
    go(d2(1, rest))
    go(d2_own(1, rest))
    got(d2(0, every))
    fin(d2_own(0, every))
    go(d3(0))
    gone(d2(0, rest))
    pack(2)
    go(d2(2, rest))
    go(d2_own(2, rest))
    got(d2(1, every))
    fin(d2_own(1, every))
    go(d3(1))
    pcp.wait()
    acc[0] = acc[0] + (prem[...] + xs[0].astype(F32))
    fin(wexp)

    def first():
        load_e(0)

    def forward():
        got(d2(2, every))
        fin(d2_own(2, every))
        go(d3(2))

    def second():
        go(r3(0))
        go(r3_own(0))
        load_e(1)

    def third():
        go(r3(1))
        go(r3_own(1))
        load_e(2)
        gone(r3(0))
        fin(r3_own(0))

    def middle():
        got(r3(0))
        go(r2(0))
    experts(((0, first), (2, forward), (4, second), (8, third), (10, middle)))
    go(r3(2))
    go(r3_own(2))

    got(r3(1))
    fin(r3_own(1))
    go(r2(1))
    load_q(0)
    acc[1:4] = jnp.zeros((3, TOK, D), F32)
    add_all(0)
    got(r3(2))
    fin(r3_own(2))
    go(r2(2))
    load_q(1)
    add_all(1)
    load_q(2)
    def last(j, _):
        i = (j + 1) % 4
        for p in range(3):
            add(2, p, i)

        @pl.when(j < 3)
        def _():
            for p in range(3):
                r1_at(p, i).start()
        return 0
    lax.fori_loop(0, 4, last, 0)
    res = local(acc.at[0], own, 0)
    res.start()
    fin([r1_at(p, i) for i in range(1, 4) for p in range(3)])
    res.wait()
    gone(d1 + d2(0, (0,)) + d2(1, every) + d2(2, every) + d3(0) + d3(1) + d3(2) + r3(1) + r3(2))
    for c in range(NC):
        gone(r2(c))


def _layer(x, idx, slot, g, ws1, ws3, ws2, w1, w3, w2):
    any_ = pl.BlockSpec(memory_space=pl.ANY)
    vm = pl.BlockSpec(memory_space=pltpu.VMEM)

    def blk(n):
        return jax.ShapeDtypeStruct((NC, 4, 4, 4, CH, n), BF)
    per = [blk(b) for _, b in COLS]
    shapes = [jax.ShapeDtypeStruct((TOK, D), F32)] + per + [blk(D)] + per + per
    shapes += [jax.ShapeDtypeStruct((4, TOK, D), F32)]
    scratch = [pltpu.VMEM((4, TOK, b), BF) for _, b in COLS]
    scratch += [pltpu.VMEM((3, 4, 8, TOK), jnp.int32), pltpu.VMEM((3, 4, 8, TOK), F32)]
    scratch += [pltpu.VMEM((8, TOK), jnp.int32), pltpu.VMEM((8, TOK), F32)]
    scratch += [pltpu.VMEM((3, TOK, 3 * TOK), BF)]
    scratch += [pltpu.VMEM((2, 3, 4, 4, CH, b), BF) for _, b in COLS]
    scratch += [pltpu.VMEM((NC, 4, 4, CH, b), BF) for _, b in COLS]
    scratch += [pltpu.VMEM((4, 4, 4, CH, D), BF)]
    scratch += [pltpu.VMEM((4, 4, 4, CH, b), BF) for _, b in COLS]
    scratch += [
        pltpu.VMEM((2, 4, 4, 4, CH, D), BF),
        pltpu.VMEM((NT, D, 256), BF),
        pltpu.VMEM((8, F, 256), BF),
        pltpu.VMEM((TOK, F), BF),
        pltpu.VMEM((4, TOK, D), F32),
        pltpu.VMEM((2, TOK, D), BF),
        pltpu.VMEM((TOK, D), F32),
        pltpu.SemaphoreType.DMA((NSEM,)),
        pltpu.SemaphoreType.DMA((NSEM,)),
        pltpu.SemaphoreType.DMA((91,)),
        pltpu.SemaphoreType.DMA((2 * NT + 8,)),
        pltpu.SemaphoreType.DMA((4,)),
    ]
    res = pl.pallas_call(
        _kernel,
        out_shape=shapes,
        in_specs=[any_, vm, vm, vm] + [any_] * 6,
        out_specs=[any_] * len(shapes),
        scratch_shapes=scratch,
        compiler_params=pltpu.CompilerParams(collective_id=0, has_side_effects=True, vmem_limit_bytes=67043328),
    )(x, idx, slot, g, ws1, ws3, ws2, w1, w3, w2)
    own, others = res[0], res[-1]
    return ((own + others[1]) + (others[2] + others[3])).astype(BF)


def solution(mesh):
    rows = P(("ep", "tp"), None)

    def body(x, idx, g, slot, ws1, ws3, ws2, w1, w3, w2):
        return _layer(x, idx.T, slot.T, g.T, ws1, ws3, ws2, w1, w3, w2)

    return jax.shard_map(
        body, mesh=mesh,
        in_specs=(rows, rows, rows, rows, P(None, "tp"), P(None, "tp"), P("tp", None),
                  P("ep", None, None), P("ep", None, None), P("ep", None, None)),
        out_specs=rows, check_vma=False)
```

time: 575 us -> 259 us (0.45)
  the two profiles are of different devices: /device:TPU:13 before, /device:TPU:0 now
where the time goes in v2:
time: 259 us
  Pallas kernels  254 us (98%)
  other arithmetic  5.11 us (2%)
    pallas_call x1, Pallas kernels, _layer(): pl.pallas_call(_kernel, out_shape=shapes, in_specs=[any_, vm, vm, vm] + [...  254 us

profile of v2, /device:TPU:0, one launch (start us, length us, event | category | flops | bytes accessed | tf_op | source)
XLA Modules:
  0.0 258.7 jit_solution(11416015465510473279)
XLA Ops:
  0.0 253.6 %shard_map.100 = (f32[256,2048]{1,0:T(8,128)}, bf16[3,4,4,4,16,640]{5,4,3,2,1,0:T(8,128)(2,1)}, bf16[3,4,4,4,16,640]{5,4,3,2,1,0:T(8,128)(2,1)}, bf16[3,4,4,4,16...) custom-call(bf16[256,2048]{1,0:T(8,128)(2,1)} %x.1, ...), custom_call_target="tpu_custom_call" | custom-call | tf_op jit(solution)/shard_map/pallas_call | solution.py:460
  253.6 5.1 %fusion = bf16[256,2048]{1,0:T(8,128)(2,1)} fusion(f32[256,2048]{1,0:T(8,128)} %get-tuple-element.7, f32[4,256,2048]{2,1,0:T(8,128)} %get-tuple-element.8), kind=kLoop, calls=%fused_computation.1 | loop fusion | flops 2097152 | bytes 9437184 | tf_op jit(solution)/shard_map/convert_element_type | solution.py:469

commit v3 on v2

--- a/solution.py
+++ b/solution.py
@@ -21,8 +21,8 @@
 COLS = ((0, 640), (640, 640), (1280, 768))
 ORDER = ((0, 1, 2), (2, 0, 1), (1, 2, 0))
 D1, PS, GS, R1, D2, D3, R3, R2 = range(8)
-BASE = {D1: 0, PS: 9, GS: 18, R1: 27, D3: 36, R3: 63, R2: 90, D2: 117}
-NSEM = 117 + 108
+BASE = {D1: 0, PS: 9, GS: 18, D3: 27, R3: 54, R2: 81, D2: 108, R1: 216}
+NSEM = 216 + 18
 
 
 def _sem(stage, c, p, i, k):
@@ -34,11 +34,13 @@
 def _kernel(x, idx, slot, g, ws1, ws3, ws2, w1, w3, w2,
             own, sa, sb, sc, e, q3a, q3b, q3c, q2a, q2b, q2c, fr,
             la, lb, lc, pt, gt, pm, gm, wt, pa, pb, pc, oa, ob, oc, ec, qa, qb, qc, r, w13, w2v, hid,
-            acc, xs, prem, ssem, rsem, lsem, wsem, tsem):
+            acc, mid, xs, prem, ssem, rsem, lsem, wsem, tsem):
     ep = lax.axis_index("ep")
     tp = lax.axis_index("tp")
-    m = (ep // 16, (ep // 4) % 4, ep % 4)
+    z0, y0, x0 = ep // 16, lax.rem(ep // 4, 4), lax.rem(ep, 4)
+    m = (z0 + tp * (y0 - z0), y0 + tp * (x0 - y0), x0 + tp * (z0 - x0))
     mz, my, mx = m
+    kz, ky, kx = 16 - 12 * tp, 4 - 3 * tp, 1 + 15 * tp
     s = (sa, sb, sc)
     q3 = (q3a, q3b, q3c)
     q2 = (q2a, q2b, q2c)
@@ -48,16 +50,18 @@
     qv = (qa, qb, qc)
     cols = tuple(pl.ds(a, b) for a, b in COLS)
 
+    AT = [[m[d] if i == 0 else lax.rem(m[d] + i, 4) for i in range(4)] for d in range(3)]
+    DEV = [[kz * (AT[0][i] if d == 0 else mz) + ky * (AT[1][i] if d == 1 else my) + kx * (AT[2][i] if d == 2 else mx)
+            for i in range(4)] for d in range(3)]
+
     def dev(d, i):
-        t = [mz, my, mx]
-        t[d] = (t[d] + i) % 4
-        return {"ep": t[0] * 16 + t[1] * 4 + t[2]}
+        return {"ep": DEV[d][i]}
 
     def at(d, i):
-        return (m[d] + i) % 4
+        return AT[d][i] if isinstance(i, int) else lax.rem(m[d] + i, 4)
 
     def src(d, i):
-        return (m[d] + 4 - i) % 4
+        return AT[d][(4 - i) % 4]
 
     def weights(u1, u3, u2):
         cps = []
@@ -155,7 +159,7 @@
 
     ri = lax.broadcasted_iota(jnp.int32, (TOK, TOK), 0)
     ra, rb, rs = ri // 64, (ri // 16) % 4, ri % 16
-    ex = (mz * 16 + ra * 4 + rb, ra * 16 + rb * 4 + mx, rb * 16 + my * 4 + ra)
+    ex = (mz * kz + ra * ky + rb * kx, ra * kz + rb * ky + mx * kx, rb * kz + my * ky + ra * kx)
     base = tuple(v * CAP + rs for v in ex)
 
     def picked(c, p, v):
@@ -170,7 +174,7 @@
     def pack(c):
         def body(k, _):
             for p in range(3):
-                pk[p][c % 2, k] = picked(c, p, (m[ORDER[p][0]] + k + 1) % 4)
+                pk[p][c % 2 if isinstance(c, int) else lax.rem(c, 2), k] = picked(c, p, at(ORDER[p][0], k + 1))
             return 0
         lax.fori_loop(0, 3, body, 0)
 
@@ -237,11 +241,11 @@
         def body(b, _):
             for at_b, event in events:
                 pl.when(b == at_b)(event)
-            z = b % 4
+            z = lax.rem(b, 4)
             up(lambda: ec[z].reshape(TOK, D), NT)
 
             def store(n, v):
-                r[(b // 4) % 2, z, :, :, :, span(n, 256)] = v.astype(BF).reshape(4, 4, CH, 256)
+                r[lax.rem(b // 4, 2), z, :, :, :, span(n, 256)] = v.astype(BF).reshape(4, 4, CH, 256)
             down(store, 8)
             return 0
         lax.fori_loop(0, 4 * NC, body, 0)
@@ -314,12 +318,22 @@
             return 0
         lax.fori_loop(0, 4, body, 0)
 
-    def r1_at(p, i):
-        d = ORDER[p][0]
-        n = BASE[R1] + p * 3 + i - 1
-        return pltpu.make_async_remote_copy(src_ref=acc.at[i, :, cols[p]], dst_ref=fr.at[i, :, cols[p]],
-                                            send_sem=ssem.at[n], recv_sem=rsem.at[n],
-                                            device_id=dev(d, i), device_id_type=MESH)
+    half = (pl.ds(0, TOK // 2), pl.ds(TOK // 2, TOK // 2))
+
+    def r1(q):
+        res = []
+        for p in range(3):
+            d = ORDER[p][0]
+            n = BASE[R1] + p * 6 + q
+            up_ = q % 2 == 0
+            if q < 2:
+                a, b = acc.at[2, half[q], cols[p]], mid.at[q, :, cols[p]]
+            else:
+                rows = half[{2: 1, 3: 0, 4: 0, 5: 1}[q]]
+                a, b = acc.at[1 if up_ else 3, rows, cols[p]], fr.at[0 if up_ else 1, rows, cols[p]]
+            res.append(pltpu.make_async_remote_copy(src_ref=a, dst_ref=b, send_sem=ssem.at[n], recv_sem=rsem.at[n],
+                                                    device_id=dev(d, 1 if up_ else 3), device_id_type=MESH))
+        return res
 
     every, rest = (0, 1, 2, 3), (1, 2, 3)
     fin(own_line)
@@ -407,19 +421,34 @@
     add_all(1)
     load_q(2)
     def last(j, _):
-        i = (j + 1) % 4
+        i = lax.rem(2 + 3 * j, 4)
         for p in range(3):
             add(2, p, i)
 
-        @pl.when(j < 3)
+        @pl.when(j == 0)
         def _():
-            for p in range(3):
-                r1_at(p, i).start()
+            go(r1(0))
+            go(r1(1))
+
+        @pl.when(j == 1)
+        def _():
+            go(r1(2))
         return 0
     lax.fori_loop(0, 4, last, 0)
+    go(r1(3))
     res = local(acc.at[0], own, 0)
     res.start()
-    fin([r1_at(p, i) for i in range(1, 4) for p in range(3)])
+    for q in range(2):
+        i = 1 + 2 * q
+        via, on = r1(q), r1(4 + q)
+        for p in range(3):
+            via[p].wait_recv()
+            acc[i, half[q], cols[p]] = acc[i, half[q], cols[p]] + mid[q, :, cols[p]]
+            on[p].start()
+    for q in range(2):
+        gone(r1(q))
+        fin(r1(2 + q))
+        fin(r1(4 + q))
     res.wait()
     gone(d1 + d2(0, (0,)) + d2(1, every) + d2(2, every) + d3(0) + d3(1) + d3(2) + r3(1) + r3(2))
     for c in range(NC):
@@ -434,7 +463,7 @@
         return jax.ShapeDtypeStruct((NC, 4, 4, 4, CH, n), BF)
     per = [blk(b) for _, b in COLS]
     shapes = [jax.ShapeDtypeStruct((TOK, D), F32)] + per + [blk(D)] + per + per
-    shapes += [jax.ShapeDtypeStruct((4, TOK, D), F32)]
+    shapes += [jax.ShapeDtypeStruct((2, TOK, D), F32)]
     scratch = [pltpu.VMEM((4, TOK, b), BF) for _, b in COLS]
     scratch += [pltpu.VMEM((3, 4, 8, TOK), jnp.int32), pltpu.VMEM((3, 4, 8, TOK), F32)]
     scratch += [pltpu.VMEM((8, TOK), jnp.int32), pltpu.VMEM((8, TOK), F32)]
@@ -449,6 +478,7 @@
         pltpu.VMEM((8, F, 256), BF),
         pltpu.VMEM((TOK, F), BF),
         pltpu.VMEM((4, TOK, D), F32),
+        pltpu.VMEM((2, TOK // 2, D), F32),
         pltpu.VMEM((2, TOK, D), BF),
         pltpu.VMEM((TOK, D), F32),
         pltpu.SemaphoreType.DMA((NSEM,)),
@@ -466,7 +496,7 @@
         compiler_params=pltpu.CompilerParams(collective_id=0, has_side_effects=True, vmem_limit_bytes=67043328),
     )(x, idx, slot, g, ws1, ws3, ws2, w1, w3, w2)
     own, others = res[0], res[-1]
-    return ((own + others[1]) + (others[2] + others[3])).astype(BF)
+    return (own + (others[0] + others[1])).astype(BF)
 
 
 def solution(mesh):

time: 259 us -> 247 us (0.954)
  Pallas kernels: 254 us -> 242 us
    pallas_call x1, Pallas kernels: 254 us -> 242 us  [_layer(): pl.pallas_call(_kernel, out_shape=shapes, in_specs=[any_, vm, vm, vm] + [...]
where the time goes in v3:
time: 247 us; the launch traced here: 246 us
  Pallas kernels  242 us (98%)
  other arithmetic  4.27 us (2%)
    pallas_call x1, Pallas kernels, _layer(): pl.pallas_call(_kernel, out_shape=shapes, in_specs=[any_, vm, vm, vm] + [...  242 us

profile of v3, /device:TPU:0, one launch (start us, length us, event | category | flops | bytes accessed | tf_op | source)
XLA Modules:
  0.0 246.5 jit_solution(13232965509125637614)
XLA Ops:
  0.0 242.2 %shard_map.100 = (f32[256,2048]{1,0:T(8,128)}, bf16[3,4,4,4,16,640]{5,4,3,2,1,0:T(8,128)(2,1)}, bf16[3,4,4,4,16,640]{5,4,3,2,1,0:T(8,128)(2,1)}, bf16[3,4,4,4,16...) custom-call(bf16[256,2048]{1,0:T(8,128)(2,1)} %x.1, ...), custom_call_target="tpu_custom_call" | custom-call | tf_op jit(solution)/shard_map/pallas_call | solution.py:490
  242.2 4.3 %fusion = bf16[256,2048]{1,0:T(8,128)(2,1)} fusion(f32[256,2048]{1,0:T(8,128)} %get-tuple-element.7, f32[2,256,2048]{2,1,0:T(8,128)} %get-tuple-element.8), kind=kLoop, calls=%fused_computation.1 | loop fusion | flops 1572864 | bytes 7340032 | tf_op jit(solution)/shard_map/convert_element_type | solution.py:499

commit v4 on v3

--- a/solution.py
+++ b/solution.py
@@ -22,7 +22,7 @@
 ORDER = ((0, 1, 2), (2, 0, 1), (1, 2, 0))
 D1, PS, GS, R1, D2, D3, R3, R2 = range(8)
 BASE = {D1: 0, PS: 9, GS: 18, D3: 27, R3: 54, R2: 81, D2: 108, R1: 216}
-NSEM = 216 + 18
+NSEM = 216 + 18 + 3
 
 
 def _sem(stage, c, p, i, k):
@@ -33,7 +33,7 @@
 
 def _kernel(x, idx, slot, g, ws1, ws3, ws2, w1, w3, w2,
             own, sa, sb, sc, e, q3a, q3b, q3c, q2a, q2b, q2c, fr,
-            la, lb, lc, pt, gt, pm, gm, wt, pa, pb, pc, oa, ob, oc, ec, qa, qb, qc, r, w13, w2v, hid,
+            la, lb, lc, iv, sv, gv, pt, gt, pm, gm, wt, pa, pb, pc, oa, ob, oc, ec, qa, qb, qc, r, w13, w2v, hid,
             acc, mid, xs, prem, ssem, rsem, lsem, wsem, tsem):
     ep = lax.axis_index("ep")
     tp = lax.axis_index("tp")
@@ -72,6 +72,10 @@
             cps.append(pltpu.make_async_copy(u2.at[:, pl.ds(n * 256, 256)], w2v.at[n], wsem.at[2 * NT + n]))
         return cps
 
+    small = [pltpu.make_async_copy(a, b, lsem.at[91 + n]) for n, (a, b) in enumerate(((idx, iv), (slot, sv), (g, gv)))]
+    for c in small:
+        c.start()
+
     bar = pltpu.get_barrier_semaphore()
     for d in range(3):
         for i in range(1, 4):
@@ -85,8 +89,10 @@
         c.start()
     pm[...] = jnp.full((8, TOK), -1, jnp.int32)
     gm[...] = jnp.zeros((8, TOK), F32)
-    pm[0:K, :] = jnp.where(slot[...] >= 0, idx[...] * CAP + slot[...], -1)
-    gm[0:K, :] = g[...]
+    for c in small:
+        c.wait()
+    pm[0:K, :] = jnp.where(sv[...] >= 0, iv[...] * CAP + sv[...], -1)
+    gm[0:K, :] = gv[...]
     for d in range(3):
         pt[d, m[d]] = pm[...]
         gt[d, m[d]] = gm[...]
@@ -118,14 +124,30 @@
 
     near = (1, 3, 2)
 
+    half = (pl.ds(0, TOK // 2), pl.ds(TOK // 2, TOK // 2))
     d1 = []
+    for i in (1, 3):
+        for p in range(3):
+            d = ORDER[p][0]
+            d1.append(remote(x.at[:, cols[p]], line[p].at[m[d]], D1, 0, p, i, dev(d, i)))
+    d1s = []
     for i in near:
         for p in range(3):
             d = ORDER[p][0]
-            d1.append(remote(pm, pt.at[d, m[d]], PS, 0, p, i, dev(d, i)))
-            d1.append(remote(gm, gt.at[d, m[d]], GS, 0, p, i, dev(d, i)))
-            d1.append(remote(x.at[:, cols[p]], line[p].at[m[d]], D1, 0, p, i, dev(d, i)))
+            d1s.append(remote(pm, pt.at[d, m[d]], PS, 0, p, i, dev(d, i)))
+            d1s.append(remote(gm, gt.at[d, m[d]], GS, 0, p, i, dev(d, i)))
+
+    def passed(q):
+        res = []
+        for p in range(3):
+            d = ORDER[p][0]
+            v = line[p].at[AT[d][3 - 2 * q], half[q]]
+            n = BASE[D1] + p * 3 + 1 if q == 0 else 234 + p
+            res.append(pltpu.make_async_remote_copy(src_ref=v, dst_ref=v, send_sem=ssem.at[n], recv_sem=rsem.at[n],
+                                                    device_id=dev(d, 1 + 2 * q), device_id_type=MESH))
+        return res
     go(d1)
+    go(d1s)
     xcp = pltpu.make_async_remote_copy(src_ref=x, dst_ref=xs.at[1], send_sem=tsem.at[0], recv_sem=tsem.at[1],
                                        device_id={"tp": 1 - tp}, device_id_type=MESH)
     xcp.start()
@@ -291,7 +313,7 @@
                 cps.append(cp)
         fin(cps)
 
-    def add(c, p, i):
+    def weigh(c, p, i):
         d = ORDER[p][0]
         v = at(d, i)
         ps = pt[d, v] - c * CH
@@ -303,10 +325,12 @@
         t = w - w1_.astype(F32)
         w2_ = t.astype(BF)
         w3_ = (t - w2_.astype(F32)).astype(BF)
-        rows = qv[p][:, :, v].reshape(TOK, COLS[p][1])
         wt[p, :, 0:TOK] = w1_
         wt[p, :, TOK:2 * TOK] = w2_
         wt[p, :, 2 * TOK:3 * TOK] = w3_
+
+    def add(p, i):
+        rows = qv[p][:, :, at(ORDER[p][0], i)].reshape(TOK, COLS[p][1])
         y = lax.dot_general(wt[p], rows, (((0,), (0,)), ((), ())), preferred_element_type=F32)
         y = (y[2 * TOK:] + y[TOK:2 * TOK]) + y[:TOK]
         acc[i, :, cols[p]] = acc[i, :, cols[p]] + y
@@ -314,11 +338,10 @@
     def add_all(c):
         def body(i, _):
             for p in range(3):
-                add(c, p, i)
+                weigh(c, p, i)
+                add(p, i)
             return 0
         lax.fori_loop(0, 4, body, 0)
-
-    half = (pl.ds(0, TOK // 2), pl.ds(TOK // 2, TOK // 2))
 
     def r1(q):
         res = []
@@ -338,10 +361,18 @@
     every, rest = (0, 1, 2, 3), (1, 2, 3)
     fin(own_line)
     pack_own()
+    go(d2(0, (0,)))
+    got(d1[0:3])
+    go(passed(0))
+    got(d1[3:6])
+    go(passed(1))
+    go(d2(1, (0,)))
+    go(d2(2, (0,)))
     for c in range(NC):
-        go(d2(c, (0,)))
         go(d2_own(c, (0,)))
-    got(d1)
+    got(d1s)
+    for q in range(2):
+        got(passed(q))
     pack(0)
     go(d2(0, rest))
     go(d2_own(0, rest))
@@ -419,22 +450,26 @@
     go(r2(2))
     load_q(1)
     add_all(1)
+    for p in range(3):
+        weigh(2, p, 2)
     load_q(2)
+    low, high = r1(0), r1(1)
+    for p in range(3):
+        add(p, 2)
+        low[p].start()
+        high[p].start()
+
     def last(j, _):
-        i = lax.rem(2 + 3 * j, 4)
-        for p in range(3):
-            add(2, p, i)
+        i = lax.rem(5 - j, 4)
+        for p in range(3):
+            weigh(2, p, i)
+            add(p, i)
 
         @pl.when(j == 0)
-        def _():
-            go(r1(0))
-            go(r1(1))
-
-        @pl.when(j == 1)
         def _():
             go(r1(2))
         return 0
-    lax.fori_loop(0, 4, last, 0)
+    lax.fori_loop(0, 3, last, 0)
     go(r1(3))
     res = local(acc.at[0], own, 0)
     res.start()
@@ -450,14 +485,13 @@
         fin(r1(2 + q))
         fin(r1(4 + q))
     res.wait()
-    gone(d1 + d2(0, (0,)) + d2(1, every) + d2(2, every) + d3(0) + d3(1) + d3(2) + r3(1) + r3(2))
+    gone(d1 + d1s + passed(0) + passed(1) + d2(0, (0,)) + d2(1, every) + d2(2, every) + d3(0) + d3(1) + d3(2) + r3(1) + r3(2))
     for c in range(NC):
         gone(r2(c))
 
 
 def _layer(x, idx, slot, g, ws1, ws3, ws2, w1, w3, w2):
     any_ = pl.BlockSpec(memory_space=pl.ANY)
-    vm = pl.BlockSpec(memory_space=pltpu.VMEM)
 
     def blk(n):
         return jax.ShapeDtypeStruct((NC, 4, 4, 4, CH, n), BF)
@@ -465,6 +499,7 @@
     shapes = [jax.ShapeDtypeStruct((TOK, D), F32)] + per + [blk(D)] + per + per
     shapes += [jax.ShapeDtypeStruct((2, TOK, D), F32)]
     scratch = [pltpu.VMEM((4, TOK, b), BF) for _, b in COLS]
+    scratch += [pltpu.VMEM((K, TOK), jnp.int32), pltpu.VMEM((K, TOK), jnp.int32), pltpu.VMEM((K, TOK), F32)]
     scratch += [pltpu.VMEM((3, 4, 8, TOK), jnp.int32), pltpu.VMEM((3, 4, 8, TOK), F32)]
     scratch += [pltpu.VMEM((8, TOK), jnp.int32), pltpu.VMEM((8, TOK), F32)]
     scratch += [pltpu.VMEM((3, TOK, 3 * TOK), BF)]
@@ -483,14 +518,14 @@
         pltpu.VMEM((TOK, D), F32),
         pltpu.SemaphoreType.DMA((NSEM,)),
         pltpu.SemaphoreType.DMA((NSEM,)),
-        pltpu.SemaphoreType.DMA((91,)),
+        pltpu.SemaphoreType.DMA((94,)),
         pltpu.SemaphoreType.DMA((2 * NT + 8,)),
         pltpu.SemaphoreType.DMA((4,)),
     ]
     res = pl.pallas_call(
         _kernel,
         out_shape=shapes,
-        in_specs=[any_, vm, vm, vm] + [any_] * 6,
+        in_specs=[any_] * 10,
         out_specs=[any_] * len(shapes),
         scratch_shapes=scratch,
         compiler_params=pltpu.CompilerParams(collective_id=0, has_side_effects=True, vmem_limit_bytes=67043328),

time: 247 us -> 242 us (0.980)
  Pallas kernels: 242 us -> 237 us
    pallas_call x1, Pallas kernels: 242 us -> 237 us  [_layer(): pl.pallas_call(_kernel, out_shape=shapes, in_specs=[any_] * 10, out_specs...]
where the time goes in v4:
time: 242 us; the launch traced here: 241 us
  Pallas kernels  237 us (98%)
  other arithmetic  4.27 us (2%)
    pallas_call x1, Pallas kernels, _layer(): pl.pallas_call(_kernel, out_shape=shapes, in_specs=[any_] * 10, out_specs...  237 us

profile of v4, /device:TPU:0, one launch (start us, length us, event | category | flops | bytes accessed | tf_op | source)
XLA Modules:
  0.0 241.3 jit_solution(7883067246131903943)
XLA Ops:
  0.0 237.0 %shard_map.100 = (f32[256,2048]{1,0:T(8,128)}, bf16[3,4,4,4,16,640]{5,4,3,2,1,0:T(8,128)(2,1)}, bf16[3,4,4,4,16,640]{5,4,3,2,1,0:T(8,128)(2,1)}, bf16[3,4,4,4,16...) custom-call(bf16[256,2048]{1,0:T(8,128)(2,1)} %x.1, ...), custom_call_target="tpu_custom_call" | custom-call | tf_op jit(solution)/shard_map/pallas_call | solution.py:525
  237.0 4.3 %fusion = bf16[256,2048]{1,0:T(8,128)(2,1)} fusion(f32[256,2048]{1,0:T(8,128)} %get-tuple-element.7, f32[2,256,2048]{2,1,0:T(8,128)} %get-tuple-element.8), kind=kLoop, calls=%fused_computation.1 | loop fusion | flops 1572864 | bytes 7340032 | tf_op jit(solution)/shard_map/convert_element_type | solution.py:534

commit v5 on v4

--- a/solution.py
+++ b/solution.py
@@ -353,7 +353,7 @@
                 a, b = acc.at[2, half[q], cols[p]], mid.at[q, :, cols[p]]
             else:
                 rows = half[{2: 1, 3: 0, 4: 0, 5: 1}[q]]
-                a, b = acc.at[1 if up_ else 3, rows, cols[p]], fr.at[0 if up_ else 1, rows, cols[p]]
+                a, b = acc.at[1 if up_ else 3, rows, cols[p]], fr.at[0 if q < 4 else 1, rows, cols[p]]
             res.append(pltpu.make_async_remote_copy(src_ref=a, dst_ref=b, send_sem=ssem.at[n], recv_sem=rsem.at[n],
                                                     device_id=dev(d, 1 if up_ else 3), device_id_type=MESH))
         return res
@@ -435,7 +435,7 @@
     def middle():
         got(r3(0))
         go(r2(0))
-    experts(((0, first), (2, forward), (4, second), (8, third), (10, middle)))
+    experts(((0, first), (2, forward), (4, second), (8, third), (9, middle)))
     go(r3(2))
     go(r3_own(2))
 
@@ -471,8 +471,6 @@
         return 0
     lax.fori_loop(0, 3, last, 0)
     go(r1(3))
-    res = local(acc.at[0], own, 0)
-    res.start()
     for q in range(2):
         i = 1 + 2 * q
         via, on = r1(q), r1(4 + q)
@@ -480,9 +478,16 @@
             via[p].wait_recv()
             acc[i, half[q], cols[p]] = acc[i, half[q], cols[p]] + mid[q, :, cols[p]]
             on[p].start()
+    got(r1(2) + r1(3))
+    res = local(fr.at[0], prem, 0)
+    res.start()
+    res.wait()
+    acc[0] = acc[0] + prem[...]
+    res = local(acc.at[0], own, 1)
+    res.start()
     for q in range(2):
         gone(r1(q))
-        fin(r1(2 + q))
+        gone(r1(2 + q))
         fin(r1(4 + q))
     res.wait()
     gone(d1 + d1s + passed(0) + passed(1) + d2(0, (0,)) + d2(1, every) + d2(2, every) + d3(0) + d3(1) + d3(2) + r3(1) + r3(2))
@@ -531,7 +536,7 @@
         compiler_params=pltpu.CompilerParams(collective_id=0, has_side_effects=True, vmem_limit_bytes=67043328),
     )(x, idx, slot, g, ws1, ws3, ws2, w1, w3, w2)
     own, others = res[0], res[-1]
-    return (own + (others[0] + others[1])).astype(BF)
+    return (own + others[1]).astype(BF)
 
 
 def solution(mesh):

time: 242 us -> 239 us (0.988)
  no operation moved by 1% of the time
where the time goes in v5:
time: 239 us
  Pallas kernels  235 us (98%)
  other arithmetic  3.46 us (1%)
    pallas_call x1, Pallas kernels, _layer(): pl.pallas_call(_kernel, out_shape=shapes, in_specs=[any_] * 10, out_specs...  235 us

profile of v5, /device:TPU:0, one launch (start us, length us, event | category | flops | bytes accessed | tf_op | source)
XLA Modules:
  0.0 238.9 jit_solution(14357577709660372210)
XLA Ops:
  0.0 235.4 %shard_map.100 = (f32[256,2048]{1,0:T(8,128)}, bf16[3,4,4,4,16,640]{5,4,3,2,1,0:T(8,128)(2,1)}, bf16[3,4,4,4,16,640]{5,4,3,2,1,0:T(8,128)(2,1)}, bf16[3,4,4,4,16...) custom-call(bf16[256,2048]{1,0:T(8,128)(2,1)} %x.1, ...), custom_call_target="tpu_custom_call" | custom-call | tf_op jit(solution)/shard_map/pallas_call | solution.py:530
  235.4 3.5 %fusion = bf16[256,2048]{1,0:T(8,128)(2,1)} fusion(f32[256,2048]{1,0:T(8,128)} %get-tuple-element.7, f32[2,256,2048]{2,1,0:T(8,128)} %get-tuple-element.8), kind=kLoop, calls=%fused_computation.1 | loop fusion | flops 1048576 | bytes 5242880 | tf_op jit(solution)/shard_map/convert_element_type | solution.py:539
